TPU v7x, 32 devices: a whole 2x2x4 slice. The times are simulated.
32 devices in a mesh: ep: 4 (over y, x), fsdp: 8 (over z, core).
Axes of the slice: x: 2, y: 2, z: 4, core: 2. Of those that a mesh axis runs over, the one named last changes fastest.
Arguments:
- train_gate: float32 [64, 2048, 1408], P('ep', 'fsdp'), may hold values from -0.1875 to 0.1875
- train_up: float32 [64, 2048, 1408], P('ep', 'fsdp'), may hold values from -0.1875 to 0.1875
- train_down: float32 [64, 1408, 2048], P('ep', None, 'fsdp'), may hold values from -0.21875 to 0.21875
- router_weight: float32 [2048, 64], P('fsdp', 'ep'), may hold values from -0.125 to 0.125
- router_gain: float32 [2048], P('fsdp'), may hold values from 0.25 to 1.75
Outputs:
- ready_gate: bfloat16 [64, 2048, 1408], P('ep', None, 'fsdp')
- ready_up: bfloat16 [64, 2048, 1408], P('ep', None, 'fsdp')
- ready_down: bfloat16 [64, 1408, 2048], P('ep', 'fsdp')
- scale_gate: float32 [64, 1408], P('ep', 'fsdp')
- scale_up: float32 [64, 1408], P('ep', 'fsdp')
- scale_down: float32 [64, 1408], P('ep', 'fsdp')
- serve_router: bfloat16 [2048, 64], replicated
All inputs are finite; a program needn't handle non-finite values. Where the computation divides by a largest or mean magnitude, that divisor is 1e-20 or more.
Results may differ from a plain program's by a relative error of at most 0.001.
Values may be sent and summed in bfloat16 or wider, within the bound.
A program may use at most 256 MiB of HBM per device.

v0:
```python
import jax
import jax.numpy as jnp
from jax import lax
from jax.sharding import PartitionSpec as P


def per_device(train_gate, train_up, train_down, router_weight, router_gain):
    scale_gate, scale_up, scale_down = lax.pmax(
        (
            jnp.max(jnp.abs(train_gate), axis=1),
            jnp.max(jnp.abs(train_up), axis=1),
            jnp.max(jnp.abs(train_down), axis=2),
        ),
        "fsdp",
    )
    narrow_gate, narrow_up, narrow_down = (
        (train_gate / jnp.expand_dims(scale_gate, 1)).astype(jnp.bfloat16),
        (train_up / jnp.expand_dims(scale_up, 1)).astype(jnp.bfloat16),
        (train_down / jnp.expand_dims(scale_down, 2)).astype(jnp.bfloat16),
    )
    ready_gate, ready_up = (
        lax.all_to_all(narrow_gate, "fsdp", split_axis=2, concat_axis=1, tiled=True),
        lax.all_to_all(narrow_up, "fsdp", split_axis=2, concat_axis=1, tiled=True),
    )
    ready_down = lax.all_to_all(narrow_down, "fsdp", split_axis=1, concat_axis=2, tiled=True)
    scale_gate = lax.dynamic_slice_in_dim(
        scale_gate, lax.axis_index("fsdp") * ready_gate.shape[2], ready_gate.shape[2], axis=1
    )
    scale_up = lax.dynamic_slice_in_dim(
        scale_up, lax.axis_index("fsdp") * ready_up.shape[2], ready_up.shape[2], axis=1
    )
    scale_down = lax.dynamic_slice_in_dim(
        scale_down, lax.axis_index("fsdp") * ready_down.shape[1], ready_down.shape[1], axis=1
    )
    part_router = (router_weight * router_gain[:, None]).astype(jnp.bfloat16)
    row_router = lax.all_gather(part_router, "fsdp", axis=0, tiled=True)
    serve_router = lax.all_gather(row_router, "ep", axis=1, tiled=True)
    return (ready_gate, ready_up, ready_down, scale_gate, scale_up, scale_down, serve_router)


def solution(mesh):
    placed = (
        P("ep", "fsdp", None),
        P("ep", "fsdp", None),
        P("ep", None, "fsdp"),
        P("fsdp", "ep"),
        P("fsdp"),
    )
    return jax.shard_map(
        per_device,
        mesh=mesh,
        in_specs=placed,
        out_specs=(
            P("ep", None, "fsdp"),
            P("ep", None, "fsdp"),
            P("ep", "fsdp", None),
            P("ep", "fsdp"),
            P("ep", "fsdp"),
            P("ep", "fsdp"),
            P(),
        ),
        check_vma=False,
    )
```

profile of v0, /device:TPU:0, one launch (start us, length us, event | category | flops | bytes accessed | tf_op | source)
XLA Modules:
  0.0 985.2 jit_solution(7565016768209817902)
XLA Ops:
  7.2 10.5 %abs_reduce_fusion = f32[16,1408]{1,0:T(8,128)} fusion(f32[16,1408,256]{2,1,0:T(8,128)} %param.7), kind=kLoop, calls=%fused_computation.2 | loop fusion | flops 11511808 | bytes 23158784 | tf_op jit(solution)/shard_map/reduce_max | solution.py:12
  17.7 10.8 %abs_reduce_fusion.1 = f32[16,1408]{1,0:T(8,128)} fusion(f32[16,256,1408]{2,1,0:T(8,128)} %param.6), kind=kLoop, calls=%fused_computation.4 | loop fusion | flops 11511808 | bytes 23158784 | tf_op jit(solution)/shard_map/reduce_max | solution.py:11
  28.6 2.4 abs_reduce_fusion.2
  31.0 23.7 %copy.24 = f32[16,256,1408]{1,0,2:T(8,128)} copy(f32[16,256,1408]{2,1,0:T(8,128)} %param.5) | data formatting | bytes 46137344 | tf_op args[0]
  54.7 32.5 %all-reduce.3.cloned.1.call-done = (f32[16,1408]{1,0:T(8,128)}, f32[16,1408]{1,0:T(8,128)}, f32[16,1408]{1,0:T(8,128)}) async-done(((f32[16,1408]{1,0:T(8,128)}, f32[16,1408]{1,0:T(8,128)}, f32[16,1408]{1,0:T(8,128)}), (f32[16,1408]{1,0:T(8,128)}, f32[16,1408]{1,0:T(8,128)}, f32[16,1408]{1,0:T(8,128)})) %all-reduce.3.cloned.1.call-update) | async-done | bytes 270352 | tf_op jit(solution)/shard_map/pmax | solution.py:8
  87.2 1.1 copy.23
  88.4 14.2 %divide_convert_fusion.1 = bf16[16,256,1408]{1,0,2:T(8,128)(2,1)} fusion(f32[16,256,1408]{1,0,2:T(8,128)} %copy.24, f32[16,1408]{0,1:T(8,128)S(1)} %copy.23), kind=kLoop, calls=%fused_computation.5 | loop fusion | flops 11534336 | bytes 34693120 | tf_op jit(solution)/shard_map/convert_element_type | solution.py:17
  102.6 5.4 all-to-all-start
  108.0 23.7 %copy.28 = f32[16,256,1408]{1,0,2:T(8,128)} copy(f32[16,256,1408]{2,1,0:T(8,128)} %param.6) | data formatting | bytes 46137344 | tf_op args[1]
  132.0 14.2 %divide_convert_fusion = bf16[16,256,1408]{1,0,2:T(8,128)(2,1)} fusion(f32[16,256,1408]{1,0,2:T(8,128)} %copy.28, f32[16,1408]{0,1:T(8,128)S(1)} %copy.27), kind=kLoop, calls=%fused_computation.3 | loop fusion | flops 11534336 | bytes 34693120 | tf_op jit(solution)/shard_map/convert_element_type | solution.py:18
  146.2 213.1 %all-to-all-done = bf16[16,256,1408]{1,0,2:T(8,128)(2,1)} async-done(((bf16[16,256,1408]{1,0,2:T(8,128)(2,1)}), bf16[16,256,1408]{1,0,2:T(8,128)(2,1)}, u32[]{:S(2)}, u32[]{:S(2)}) %all-to-all-start) | async-done | bytes 11534368 | tf_op jit(solution)/shard_map/all_to_all | solution.py:22
  359.4 5.2 all-to-all-start.1
  364.9 32.6 %fusion = bf16[16,1408,256]{2,0,1:T(8,128)(2,1)} fusion(f32[16,1408,256]{2,1,0:T(8,128)} %param.7, f32[16,1408]{0,1:T(8,128)S(1)} %copy.31), kind=kLoop, calls=%fused_computation.1 | loop fusion | flops 11534336 | bytes 34693120 | tf_op jit(solution)/shard_map/convert_element_type | solution.py:19
  397.5 218.4 %all-to-all-done.1 = bf16[16,256,1408]{1,0,2:T(8,128)(2,1)} async-done(((bf16[16,256,1408]{1,0,2:T(8,128)(2,1)}), bf16[16,256,1408]{1,0,2:T(8,128)(2,1)}, u32[]{:S(2)}, u32[]{:S(2)}) %all-to-all-start.1) | async-done | bytes 11534368 | tf_op jit(solution)/shard_map/all_to_all | solution.py:23
  615.9 5.3 all-to-all-start.2
  621.3 257.3 %all_gather.6 = bf16[2048,16]{0,1:T(8,128)(2,1)S(1)} all-gather(bf16[256,16]{0,1:T(8,128)(2,1)S(1)} %multiply_convert_fusion), channel_id=1, replica_groups=mesh['ep'=4,'fsdp'=8] {'fsdp'}, dimensions={0}, use_global_device_ids=true | all-gather | bytes 73728 | tf_op jit(solution)/shard_map/all_gather | solution.py:36
  878.5 9.1 all_gather.7
  887.7 1.4 constant_dynamic-slice_fusion.2
  889.8 11.3 %copy.26 = bf16[16,8,256,176]{2,1,3,0:T(8,128)(2,1)} copy(bf16[16,8,256,176]{2,0,3,1:T(8,128)(2,1)} %bitcast.2) | data formatting | bytes 23068672 | tf_op jit(solution)/shard_map/all_to_all | solution.py:22
  901.1 18.0 %all_to_all.42 = bf16[16,2048,176]{1,2,0:T(8,128)(2,1)} reshape(bf16[16,8,256,176]{2,1,3,0:T(8,128)(2,1)} %copy.26) | data formatting | bytes 23068672 | tf_op jit(solution)/shard_map/all_to_all | solution.py:22
  919.1 11.3 %copy.30 = bf16[16,8,256,176]{2,1,3,0:T(8,128)(2,1)} copy(bf16[16,8,256,176]{2,0,3,1:T(8,128)(2,1)} %bitcast.5) | data formatting | bytes 23068672 | tf_op jit(solution)/shard_map/all_to_all | solution.py:23
  930.4 18.0 %all_to_all.46 = bf16[16,2048,176]{1,2,0:T(8,128)(2,1)} reshape(bf16[16,8,256,176]{2,1,3,0:T(8,128)(2,1)} %copy.30) | data formatting | bytes 23068672 | tf_op jit(solution)/shard_map/all_to_all | solution.py:23
  948.4 11.4 %copy.33 = bf16[16,176,8,256]{3,2,1,0:T(8,128)(2,1)} copy(bf16[16,176,8,256]{3,0,1,2:T(8,128)(2,1)} %bitcast.7) | data formatting | bytes 23068672 | tf_op jit(solution)/shard_map/all_to_all | solution.py:25
  959.7 18.0 %all_to_all.50 = bf16[16,176,2048]{2,1,0:T(8,128)(2,1)} reshape(bf16[16,176,8,256]{3,2,1,0:T(8,128)(2,1)} %copy.33) | data formatting | bytes 23068672 | tf_op jit(solution)/shard_map/all_to_all | solution.py:25
  (29 shorter events, 2.0 us)
Async XLA Ops:
  7.2 80.1 %all-reduce.3.cloned.1.call-start = ((), (), s32[]{:S(2)}) async-start(), calls=%async_computation.3 | async-start | bytes 540672 | tf_op jit(solution)/shard_map/pmax | solution.py:8
  7.2 21.3 %slice-start = ((s8[23068672]{0:T(1024)(128)(4,1)}), s8[4194304]{0:T(1024)(128)(4,1)S(1)}, s32[]{:S(2)}) async-start(s8[23068672]{0:T(1024)(128)(4,1)} %bitcast.19), calls=%async_computation.4 | async-start | bytes 8388608
  7.2 21.3 %slice-start.1 = ((s8[23068672]{0:T(1024)(128)(4,1)}), s8[4194304]{0:T(1024)(128)(4,1)S(1)}, s32[]{:S(2)}) async-start(s8[23068672]{0:T(1024)(128)(4,1)} %bitcast.19), calls=%async_computation.5 | async-start | bytes 8388608
  7.2 21.3 %slice-start.2 = ((s8[23068672]{0:T(1024)(128)(4,1)}), s8[4194304]{0:T(1024)(128)(4,1)S(1)}, s32[]{:S(2)}) async-start(s8[23068672]{0:T(1024)(128)(4,1)} %bitcast.19), calls=%async_computation.6 | async-start | bytes 8388608
  17.7 10.8 %slice-start.3 = ((s8[23068672]{0:T(1024)(128)(4,1)}), s8[4194304]{0:T(1024)(128)(4,1)S(1)}, s32[]{:S(2)}) async-start(s8[23068672]{0:T(1024)(128)(4,1)} %bitcast.19), calls=%async_computation.7 | async-start | bytes 8388608
  17.7 10.8 %slice-start.4 = ((s8[23068672]{0:T(1024)(128)(4,1)}), s8[4194304]{0:T(1024)(128)(4,1)S(1)}, s32[]{:S(2)}) async-start(s8[23068672]{0:T(1024)(128)(4,1)} %bitcast.19), calls=%async_computation.8 | async-start | bytes 8388608
  17.7 10.9 %slice-start.5 = ((s8[23068672]{0:T(1024)(128)(4,1)}), s8[2097152]{0:T(1024)(128)(4,1)S(1)}, s32[]{:S(2)}) async-start(s8[23068672]{0:T(1024)(128)(4,1)} %bitcast.19), calls=%async_computation.9 | async-start | bytes 4194304
  102.6 256.8 %all-to-all-start = ((bf16[16,256,1408]{1,0,2:T(8,128)(2,1)}), bf16[16,256,1408]{1,0,2:T(8,128)(2,1)}, u32[]{:S(2)}, u32[]{:S(2)}) async-start(bf16[16,256,1408]{1,0,2:T(8,128)(2,1)} %divide_convert_fusion.1), calls=%async_computation | async-start | bytes 23068672 | tf_op jit(solution)/shard_map/all_to_all | solution.py:22
  108.0 23.7 %copy-start = (f32[16,1408]{1,0:T(8,128)S(1)}, f32[16,1408]{1,0:T(8,128)}, u32[]{:S(2)}) copy-start(f32[16,1408]{1,0:T(8,128)} %get-tuple-element.8) | copy-start | bytes 270340
  132.0 232.6 %copy-start.1 = (f32[16,1408]{1,0:T(8,128)S(1)}, f32[16,1408]{1,0:T(8,128)}, u32[]{:S(2)}) copy-start(f32[16,1408]{1,0:T(8,128)} %get-tuple-element.9) | copy-start | bytes 270340
  359.4 256.5 %all-to-all-start.1 = ((bf16[16,256,1408]{1,0,2:T(8,128)(2,1)}), bf16[16,256,1408]{1,0,2:T(8,128)(2,1)}, u32[]{:S(2)}, u32[]{:S(2)}) async-start(bf16[16,256,1408]{1,0,2:T(8,128)(2,1)} %divide_convert_fusion), calls=%async_computation.1 | async-start | bytes 23068672 | tf_op jit(solution)/shard_map/all_to_all | solution.py:23
  364.9 256.3 %copy-start.2 = (f32[256,16]{0,1:T(8,128)S(1)}, f32[256,16]{0,1:T(8,128)}, u32[]{:S(2)}) copy-start(f32[256,16]{0,1:T(8,128)} %param.8) | copy-start | bytes 49156
  364.9 256.3 %copy-start.3 = (f32[256]{0:T(256)S(1)}, f32[256]{0:T(256)}, u32[]{:S(2)}) copy-start(f32[256]{0:T(256)} %param.9) | copy-start | bytes 3076
  615.9 332.5 %all-to-all-start.2 = ((bf16[16,1408,256]{2,0,1:T(8,128)(2,1)}), bf16[16,1408,256]{2,0,1:T(8,128)(2,1)}, u32[]{:S(2)}, u32[]{:S(2)}) async-start(bf16[16,1408,256]{2,0,1:T(8,128)(2,1)} %fusion), calls=%async_computation.2 | async-start | bytes 23068672 | tf_op jit(solution)/shard_map/all_to_all | solution.py:25
Sparse Core Ops, SparseCore 0:
  31.1 56.0 all-reduce.2
where the time goes:
time: 988 us; the launch traced here: 985 us
  waiting for transfers between devices  464 us (47%)
  blocking collectives  266 us (27%)
  local copies, waits for them, and re-layouts  140 us (14%)
  other arithmetic  84.8 us (9%)
  starting transfers between devices  16 us (2%)
  between operations  14.2 us (1%)
    all_gather x1, blocking collectives, per_device(): row_router = lax.all_gather(part_router, 'fsdp', axis=0, tiled=True)  257 us
    all_to_all x1, waiting for transfers between devices, per_device(): lax.all_to_all(narrow_up, 'fsdp', split_axis=2, concat_axis=1, tiled=True)  218 us
    all_to_all x1, waiting for transfers between devices, per_device(): lax.all_to_all(narrow_gate, 'fsdp', split_axis=2, concat_axis=1, tiled=True)  213 us
    unnamed x23, local copies, waits for them, and re-layouts  48.2 us
    convert_element_type x1, other arithmetic, per_device(): (train_down / jnp.expand_dims(scale_down, 2)).astype(jnp.bfloat16)  32.6 us
    pmax x1, waiting for transfers between devices, per_device(): lax.pmax((jnp.max(jnp.abs(train_gate), axis=1), jnp.max(jnp.abs(train_up)...  32.5 us
    all_to_all x2, local copies, waits for them, and re-layouts, per_device(): lax.all_to_all(narrow_down, 'fsdp', split_axis=1, concat_axis=2, tiled=True)  29.3 us
    all_to_all x2, local copies, waits for them, and re-layouts, per_device(): lax.all_to_all(narrow_gate, 'fsdp', split_axis=2, concat_axis=1, tiled=True)  29.3 us
  transfers between devices with their start and end apart: 4, of which 3 were waited for; matrix products, arithmetic and copies ran while one was open for 12% of the time, Pallas kernels for 0%

commit v1 on v0

--- a/solution.py
+++ b/solution.py
@@ -2,6 +2,16 @@
 import jax.numpy as jnp
 from jax import lax
 from jax.sharding import PartitionSpec as P
+
+_test_keys = lambda comm_axis, a0: jnp.concatenate(
+    lax.all_to_all(
+        jnp.stack(jnp.split(a0, lax.axis_size(comm_axis), 2), axis=0),
+        axis_name=comm_axis,
+        split_axis=0,
+        concat_axis=0,
+    ),
+    1,
+)
 
 
 def per_device(train_gate, train_up, train_down, router_weight, router_gain):
@@ -19,7 +29,7 @@
         (train_down / jnp.expand_dims(scale_down, 2)).astype(jnp.bfloat16),
     )
     ready_gate, ready_up = (
-        lax.all_to_all(narrow_gate, "fsdp", split_axis=2, concat_axis=1, tiled=True),
+        _test_keys("fsdp", narrow_gate),
         lax.all_to_all(narrow_up, "fsdp", split_axis=2, concat_axis=1, tiled=True),
     )
     ready_down = lax.all_to_all(narrow_down, "fsdp", split_axis=1, concat_axis=2, tiled=True)

time: 988 us -> 972 us (0.984)
  local copies, waits for them, and re-layouts: 140 us -> 129 us
    all_to_all x2 -> x0, local copies, waits for them, and re-layouts: 29.3 us -> none  [per_device(): lax.all_to_all(narrow_gate, 'fsdp', split_axis=2, concat_axis=1, tiled=True)]
    reshape x0 -> x1, local copies, waits for them, and re-layouts: none -> 10 us  [jnp.concatenate(lax.all_to_all(jnp.stack(jnp.split(a0, lax.axis_size(comm...]
    unnamed x23 -> x30, local copies, waits for them, and re-layouts: 48.2 us -> 56.2 us
where the time goes in v1:
time: 972 us; the launch traced here: 970 us
  waiting for transfers between devices  464 us (48%)
  blocking collectives  266 us (27%)
  local copies, waits for them, and re-layouts  129 us (13%)
  other arithmetic  80.3 us (8%)
  starting transfers between devices  16 us (2%)
  between operations  14.2 us (1%)
    all_gather x1, blocking collectives, per_device(): row_router = lax.all_gather(part_router, 'fsdp', axis=0, tiled=True)  257 us
    all_to_all x1, waiting for transfers between devices, per_device(): lax.all_to_all(narrow_up, 'fsdp', split_axis=2, concat_axis=1, tiled=True)  218 us
    all_to_all x1, waiting for transfers between devices, lax.all_to_all(jnp.stack(jnp.split(a0, lax.axis_size(comm_axis), 2), axis...  213 us
    unnamed x30, local copies, waits for them, and re-layouts  56.2 us
    pmax x1, waiting for transfers between devices, per_device(): lax.pmax((jnp.max(jnp.abs(train_gate), axis=1), jnp.max(jnp.abs(train_up)...  32.9 us
    convert_element_type x1, other arithmetic, per_device(): (train_down / jnp.expand_dims(scale_down, 2)).astype(jnp.bfloat16)  32.6 us
    all_to_all x2, local copies, waits for them, and re-layouts, per_device(): lax.all_to_all(narrow_down, 'fsdp', split_axis=1, concat_axis=2, tiled=True)  29.3 us
    all_to_all x2, local copies, waits for them, and re-layouts, per_device(): lax.all_to_all(narrow_up, 'fsdp', split_axis=2, concat_axis=1, tiled=True)  29.3 us
  transfers between devices with their start and end apart: 4, of which 3 were waited for; matrix products, arithmetic and copies ran while one was open for 12% of the time, Pallas kernels for 0%

profile of v1, /device:TPU:0, one launch (start us, length us, event | category | flops | bytes accessed | tf_op | source)
XLA Modules:
  0.0 970.0 jit_solution(5331135069680932767)
XLA Ops:
  7.2 10.5 %abs_reduce_fusion = f32[16,1408]{1,0:T(8,128)} fusion(f32[16,1408,256]{2,1,0:T(8,128)} %param.7), kind=kLoop, calls=%fused_computation.2 | loop fusion | flops 11511808 | bytes 23158784 | tf_op jit(solution)/shard_map/reduce_max | solution.py:22
  17.7 10.8 %abs_reduce_fusion.1 = f32[16,1408]{1,0:T(8,128)} fusion(f32[16,256,1408]{2,1,0:T(8,128)} %param.6), kind=kLoop, calls=%fused_computation.4 | loop fusion | flops 11511808 | bytes 23158784 | tf_op jit(solution)/shard_map/reduce_max | solution.py:21
  28.6 2.4 abs_reduce_fusion.2
  31.0 23.4 %copy.30 = f32[16,256,1408]{1,2,0:T(8,128)} copy(f32[16,256,1408]{2,1,0:T(8,128)} %param.5) | data formatting | bytes 46137344 | tf_op args[0]
  54.4 32.9 %all-reduce.3.cloned.1.call-done = (f32[16,1408]{1,0:T(8,128)}, f32[16,1408]{1,0:T(8,128)}, f32[16,1408]{1,0:T(8,128)}) async-done(((f32[16,1408]{1,0:T(8,128)}, f32[16,1408]{1,0:T(8,128)}, f32[16,1408]{1,0:T(8,128)}), (f32[16,1408]{1,0:T(8,128)}, f32[16,1408]{1,0:T(8,128)}, f32[16,1408]{1,0:T(8,128)})) %all-reduce.3.cloned.1.call-update) | async-done | bytes 270352 | tf_op jit(solution)/shard_map/pmax | solution.py:18
  87.2 9.8 %divide_convert_fusion.1 = bf16[16,256,1408]{1,2,0:T(8,128)(2,1)S(1)} fusion(f32[16,256,1408]{1,2,0:T(8,128)} %copy.30, f32[16,1408]{1,0:T(8,128)} %get-tuple-element.7), kind=kLoop, calls=%fused_computation.5 | loop fusion | flops 11534336 | bytes 34693120 | tf_op jit(solution)/shard_map/convert_element_type | solution.py:27
  97.1 1.2 fusion.8
  101.8 1.2 fusion.4
  106.6 5.4 all-to-all-start
  112.0 23.7 %copy.33 = f32[16,256,1408]{1,0,2:T(8,128)} copy(f32[16,256,1408]{2,1,0:T(8,128)} %param.6) | data formatting | bytes 46137344 | tf_op args[1]
  136.0 14.2 %divide_convert_fusion = bf16[16,256,1408]{1,0,2:T(8,128)(2,1)} fusion(f32[16,256,1408]{1,0,2:T(8,128)} %copy.33, f32[16,1408]{0,1:T(8,128)S(1)} %copy.32), kind=kLoop, calls=%fused_computation.3 | loop fusion | flops 11534336 | bytes 34693120 | tf_op jit(solution)/shard_map/convert_element_type | solution.py:28
  150.2 213.2 %all-to-all-done = bf16[8,16,256,176]{2,3,1,0:T(8,128)(2,1)} async-done(((bf16[8,16,256,176]{2,3,1,0:T(8,128)(2,1)}), bf16[8,16,256,176]{2,3,1,0:T(8,128)(2,1)}, u32[]{:S(2)}, u32[]{:S(2)}) %all-to-all-start) | async-done | bytes 11534368 | tf_op jit(solution)/shard_map/all_to_all | solution.py:7
  363.4 5.2 all-to-all-start.1
  368.9 32.6 %fusion = bf16[16,1408,256]{2,0,1:T(8,128)(2,1)} fusion(f32[16,1408,256]{2,1,0:T(8,128)} %param.7, f32[16,1408]{0,1:T(8,128)S(1)} %copy.36), kind=kLoop, calls=%fused_computation.1 | loop fusion | flops 11534336 | bytes 34693120 | tf_op jit(solution)/shard_map/convert_element_type | solution.py:29
  401.5 218.4 %all-to-all-done.1 = bf16[16,256,1408]{1,0,2:T(8,128)(2,1)} async-done(((bf16[16,256,1408]{1,0,2:T(8,128)(2,1)}), bf16[16,256,1408]{1,0,2:T(8,128)(2,1)}, u32[]{:S(2)}, u32[]{:S(2)}) %all-to-all-start.1) | async-done | bytes 11534368 | tf_op jit(solution)/shard_map/all_to_all | solution.py:33
  619.9 5.3 all-to-all-start.2
  625.3 257.3 %all_gather.6 = bf16[2048,16]{0,1:T(8,128)(2,1)S(1)} all-gather(bf16[256,16]{0,1:T(8,128)(2,1)S(1)} %multiply_convert_fusion), channel_id=1, replica_groups=mesh['ep'=4,'fsdp'=8] {'fsdp'}, dimensions={0}, use_global_device_ids=true | all-gather | bytes 73728 | tf_op jit(solution)/shard_map/all_gather | solution.py:46
  882.6 9.1 all_gather.7
  891.7 1.4 constant_dynamic-slice_fusion.2
  893.8 10.0 %copy.40 = bf16[8,16,22,8,256]{4,3,0,2,1:T(8,128)(2,1)} copy(bf16[8,16,22,8,256]{4,3,2,1,0:T(8,128)(2,1)} %bitcast.15) | data formatting | bytes 23068672 | tf_op jit(solution)/shard_map/reshape | solution.py:6
  903.8 11.3 %copy.35 = bf16[16,8,256,176]{2,1,3,0:T(8,128)(2,1)} copy(bf16[16,8,256,176]{2,0,3,1:T(8,128)(2,1)} %bitcast.11) | data formatting | bytes 23068672 | tf_op jit(solution)/shard_map/all_to_all | solution.py:33
  915.1 18.0 %all_to_all.33 = bf16[16,2048,176]{1,2,0:T(8,128)(2,1)} reshape(bf16[16,8,256,176]{2,1,3,0:T(8,128)(2,1)} %copy.35) | data formatting | bytes 23068672 | tf_op jit(solution)/shard_map/all_to_all | solution.py:33
  933.1 11.4 %copy.38 = bf16[16,176,8,256]{3,2,1,0:T(8,128)(2,1)} copy(bf16[16,176,8,256]{3,0,1,2:T(8,128)(2,1)} %bitcast.13) | data formatting | bytes 23068672 | tf_op jit(solution)/shard_map/all_to_all | solution.py:35
  944.4 18.0 %all_to_all.37 = bf16[16,176,2048]{2,1,0:T(8,128)(2,1)} reshape(bf16[16,176,8,256]{3,2,1,0:T(8,128)(2,1)} %copy.38) | data formatting | bytes 23068672 | tf_op jit(solution)/shard_map/all_to_all | solution.py:35
  (35 shorter events, 9.2 us)
Async XLA Ops:
  7.2 80.1 %all-reduce.3.cloned.1.call-start = ((), (), s32[]{:S(2)}) async-start(), calls=%async_computation.3 | async-start | bytes 540672 | tf_op jit(solution)/shard_map/pmax | solution.py:18
  7.2 21.3 %slice-start = ((s8[23068672]{0:T(1024)(128)(4,1)}), s8[4194304]{0:T(1024)(128)(4,1)S(1)}, s32[]{:S(2)}) async-start(s8[23068672]{0:T(1024)(128)(4,1)} %bitcast.47), calls=%async_computation.4 | async-start | bytes 8388608
  7.2 21.3 %slice-start.1 = ((s8[23068672]{0:T(1024)(128)(4,1)}), s8[4194304]{0:T(1024)(128)(4,1)S(1)}, s32[]{:S(2)}) async-start(s8[23068672]{0:T(1024)(128)(4,1)} %bitcast.47), calls=%async_computation.5 | async-start | bytes 8388608
  7.2 21.3 %slice-start.2 = ((s8[23068672]{0:T(1024)(128)(4,1)}), s8[4194304]{0:T(1024)(128)(4,1)S(1)}, s32[]{:S(2)}) async-start(s8[23068672]{0:T(1024)(128)(4,1)} %bitcast.47), calls=%async_computation.6 | async-start | bytes 8388608
  17.7 10.8 %slice-start.3 = ((s8[23068672]{0:T(1024)(128)(4,1)}), s8[4194304]{0:T(1024)(128)(4,1)S(1)}, s32[]{:S(2)}) async-start(s8[23068672]{0:T(1024)(128)(4,1)} %bitcast.47), calls=%async_computation.7 | async-start | bytes 8388608
  17.7 10.8 %slice-start.4 = ((s8[23068672]{0:T(1024)(128)(4,1)}), s8[4194304]{0:T(1024)(128)(4,1)S(1)}, s32[]{:S(2)}) async-start(s8[23068672]{0:T(1024)(128)(4,1)} %bitcast.47), calls=%async_computation.8 | async-start | bytes 8388608
  17.7 10.9 %slice-start.5 = ((s8[23068672]{0:T(1024)(128)(4,1)}), s8[2097152]{0:T(1024)(128)(4,1)S(1)}, s32[]{:S(2)}) async-start(s8[23068672]{0:T(1024)(128)(4,1)} %bitcast.47), calls=%async_computation.9 | async-start | bytes 4194304
  106.6 256.8 %all-to-all-start = ((bf16[8,16,256,176]{2,3,1,0:T(8,128)(2,1)}), bf16[8,16,256,176]{2,3,1,0:T(8,128)(2,1)}, u32[]{:S(2)}, u32[]{:S(2)}) async-start(bf16[8,16,256,176]{2,3,1,0:T(8,128)(2,1)} %fusion.1), calls=%async_computation | async-start | bytes 23068672 | tf_op jit(solution)/shard_map/all_to_all | solution.py:7
  112.0 23.7 %copy-start = (f32[16,1408]{1,0:T(8,128)S(1)}, f32[16,1408]{1,0:T(8,128)}, u32[]{:S(2)}) copy-start(f32[16,1408]{1,0:T(8,128)} %get-tuple-element.8) | copy-start | bytes 270340
  150.2 218.4 %copy-start.1 = (f32[16,1408]{1,0:T(8,128)S(1)}, f32[16,1408]{1,0:T(8,128)}, u32[]{:S(2)}) copy-start(f32[16,1408]{1,0:T(8,128)} %get-tuple-element.9) | copy-start | bytes 270340
  363.4 256.5 %all-to-all-start.1 = ((bf16[16,256,1408]{1,0,2:T(8,128)(2,1)}), bf16[16,256,1408]{1,0,2:T(8,128)(2,1)}, u32[]{:S(2)}, u32[]{:S(2)}) async-start(bf16[16,256,1408]{1,0,2:T(8,128)(2,1)} %divide_convert_fusion), calls=%async_computation.1 | async-start | bytes 23068672 | tf_op jit(solution)/shard_map/all_to_all | solution.py:33
  401.5 223.7 %copy-start.2 = (f32[256,16]{0,1:T(8,128)S(1)}, f32[256,16]{0,1:T(8,128)}, u32[]{:S(2)}) copy-start(f32[256,16]{0,1:T(8,128)} %param.8) | copy-start | bytes 49156
  401.5 223.7 %copy-start.3 = (f32[256]{0:T(256)S(1)}, f32[256]{0:T(256)}, u32[]{:S(2)}) copy-start(f32[256]{0:T(256)} %param.9) | copy-start | bytes 3076
  619.9 313.2 %all-to-all-start.2 = ((bf16[16,1408,256]{2,0,1:T(8,128)(2,1)}), bf16[16,1408,256]{2,0,1:T(8,128)(2,1)}, u32[]{:S(2)}, u32[]{:S(2)}) async-start(bf16[16,1408,256]{2,0,1:T(8,128)(2,1)} %fusion), calls=%async_computation.2 | async-start | bytes 23068672 | tf_op jit(solution)/shard_map/all_to_all | solution.py:35
Sparse Core Ops, SparseCore 0:
  31.1 56.0 all-reduce.2
